TPU v7x, 32 devices: a whole 2x2x4 slice. The times are simulated.
32 devices in a mesh: dp: 4 (over x, y), cp: 8 (over z, core).
Axes of the slice: x: 2, y: 2, z: 4, core: 2. Of those that a mesh axis runs over, the one named last changes fastest.
Arguments:
- hidden: bfloat16 [12, 3072, 1792], P('dp', 'cp'), parts along dimension 0
- lengths: int32 [12], P('dp'), parts along dimension 0
- w_qkv: bfloat16 [3, 1792, 5376], replicated
- w_out: bfloat16 [3, 1792, 1792], replicated
- w_in: bfloat16 [3, 1792, 7680], replicated
- w_mlp_out: bfloat16 [3, 3840, 1792], replicated
- attn_gamma: float32 [3, 1792], replicated
- mlp_gamma: float32 [3, 1792], replicated
Outputs:
- output: bfloat16 [12, 3072, 1792], P('dp', 'cp'), parts along dimension 0
There are 4 independent parts. A program takes and returns all parts, laid end to end along the dimension named above; an argument that names none is the same for every part.
All inputs are finite; a program needn't handle non-finite values.
Results may differ from a plain program's by a relative error of at most 0.0149993.
Values are sent between devices in bfloat16 or wider.
A program may use at most 1 GiB of HBM per device.

v0:
```python
import jax
import jax.numpy as jnp
from jax import lax
from jax.sharding import PartitionSpec as P

HEAD_DIM = 64
WINDOW_HALF = 64
QUERY_BLOCK = 128
THETA_LOCAL = 10000.0
THETA_GLOBAL = 160000.0
LN_EPS = 1e-5
LAYER_GLOBAL = (False, False, True)


def layer_norm(resid, gamma):
    resid_f32 = resid.astype(jnp.float32)
    row_mean = jnp.mean(resid_f32, axis=-1, keepdims=True)
    centered = resid_f32 - row_mean
    row_var = jnp.mean(centered * centered, axis=-1, keepdims=True)
    return (centered * lax.rsqrt(row_var + LN_EPS) * gamma).astype(jnp.bfloat16)


def apply_rope(heads_in, positions, rope_theta):
    half_dim = HEAD_DIM // 2
    inv_freq = rope_theta ** (-jnp.arange(0, HEAD_DIM, 2, dtype=jnp.float32) / HEAD_DIM)
    angles = positions.astype(jnp.float32)[:, None] * inv_freq[None, :]
    cos_tab = jnp.cos(angles)[:, None, :]
    sin_tab = jnp.sin(angles)[:, None, :]
    heads_f32 = heads_in.astype(jnp.float32)
    first_half = heads_f32[..., :half_dim]
    second_half = heads_f32[..., half_dim:]
    return jnp.concatenate([first_half * cos_tab - second_half * sin_tab, second_half * cos_tab + first_half * sin_tab], axis=-1).astype(jnp.bfloat16)


def masked_softmax(scores, allowed):
    scores = jnp.where(allowed, scores, -1e30)
    row_max = jnp.max(scores, axis=-1, keepdims=True)
    exp_scores = jnp.exp(scores - row_max)
    return (exp_scores / jnp.sum(exp_scores, axis=-1, keepdims=True)).astype(jnp.bfloat16)


def finish_rows(attn_out, seq_offset, lengths):
    row_pos = seq_offset + jnp.arange(attn_out.shape[1])
    row_ok = row_pos[None, :, None] < lengths[:, None, None]
    return jnp.where(row_ok, attn_out, 0.0).astype(jnp.bfloat16)


def local_attention(queries, key_val_ext, seq_offset, lengths):
    num_docs, chunk_len, num_heads = queries.shape[:3]
    n_blocks = chunk_len // QUERY_BLOCK
    span_len = 2 * QUERY_BLOCK
    query_blocks = queries.reshape(num_docs, n_blocks, QUERY_BLOCK, num_heads, HEAD_DIM)
    lower_half = key_val_ext[:, :chunk_len].reshape(num_docs, n_blocks, QUERY_BLOCK, 2, num_heads, HEAD_DIM)
    upper_half = key_val_ext[:, QUERY_BLOCK:QUERY_BLOCK + chunk_len].reshape(num_docs, n_blocks, QUERY_BLOCK, 2, num_heads, HEAD_DIM)
    kv_blocks = jnp.concatenate([lower_half, upper_half], axis=2)
    scores = jnp.einsum('bnqhd,bnkhd->bnhqk', query_blocks, kv_blocks[:, :, :, 0], preferred_element_type=jnp.float32) * HEAD_DIM ** -0.5
    row_idx = jnp.arange(QUERY_BLOCK)[:, None]
    col_idx = jnp.arange(span_len)[None, :]
    in_window = (col_idx >= row_idx) & (col_idx <= row_idx + 2 * WINDOW_HALF)
    key_pos = seq_offset - WINDOW_HALF + jnp.arange(n_blocks)[:, None] * QUERY_BLOCK + col_idx
    key_ok = (key_pos >= 0)[None] & (key_pos[None] < lengths[:, None, None])
    allowed = in_window[None, None, None] & key_ok[:, :, None, None, :]
    attn_probs = masked_softmax(scores, allowed)
    attn_out = jnp.einsum('bnhqk,bnkhd->bnqhd', attn_probs, kv_blocks[:, :, :, 1], preferred_element_type=jnp.float32)
    return finish_rows(attn_out.reshape(num_docs, chunk_len, num_heads * HEAD_DIM), seq_offset, lengths)


def global_attention(queries, key_val_all, seq_offset, lengths):
    num_docs, chunk_len, num_heads = queries.shape[:3]
    total_len = key_val_all.shape[1]
    n_blocks = chunk_len // QUERY_BLOCK
    query_blocks = jnp.moveaxis(queries.reshape(num_docs, n_blocks, QUERY_BLOCK, num_heads, HEAD_DIM), 1, 0)
    keys_all = key_val_all[:, :, 0]
    values_all = key_val_all[:, :, 1]
    key_ok = (jnp.arange(total_len)[None, :] < lengths[:, None])[:, None, None, :]

    def one_block(block_queries):
        scores = jnp.einsum('bqhd,bkhd->bhqk', block_queries, keys_all, preferred_element_type=jnp.float32) * HEAD_DIM ** -0.5
        attn_probs = masked_softmax(scores, key_ok)
        return jnp.einsum('bhqk,bkhd->bqhd', attn_probs, values_all, preferred_element_type=jnp.float32)

    block_outs = lax.map(one_block, query_blocks)
    attn_out = jnp.moveaxis(block_outs, 0, 1).reshape(num_docs, chunk_len, num_heads * HEAD_DIM)
    return finish_rows(attn_out, seq_offset, lengths)


def project_qkv(resid, gamma, w_qkv_layer, positions, rope_theta):
    num_docs, seq_count, d_model = resid.shape
    normed = layer_norm(resid, gamma)
    qkv_proj = jnp.einsum('bsd,de->bse', normed, w_qkv_layer, preferred_element_type=jnp.float32).astype(jnp.bfloat16).reshape(num_docs, seq_count, 3, d_model // HEAD_DIM, HEAD_DIM)
    queries = apply_rope(qkv_proj[:, :, 0], positions, rope_theta)
    keys_rot = apply_rope(qkv_proj[:, :, 1], positions, rope_theta)
    return queries, jnp.stack([keys_rot, qkv_proj[:, :, 2]], axis=2)


def add_attention(resid, attn_out, w_out_layer):
    update = jnp.einsum('bsd,de->bse', attn_out, w_out_layer, preferred_element_type=jnp.float32)
    return (resid.astype(jnp.float32) + update).astype(jnp.bfloat16)


def mlp_block(resid, gamma, w_in_layer, w_mlp_out_layer):
    normed = layer_norm(resid, gamma)
    up_proj = jnp.einsum('bsd,de->bse', normed, w_in_layer, preferred_element_type=jnp.float32).astype(jnp.bfloat16)
    ff_width = w_mlp_out_layer.shape[0]
    gated_act = (jax.nn.gelu(up_proj[..., :ff_width].astype(jnp.float32), approximate=False) * up_proj[..., ff_width:].astype(jnp.float32)).astype(jnp.bfloat16)
    update = jnp.einsum('bsf,fd->bsd', gated_act, w_mlp_out_layer, preferred_element_type=jnp.float32)
    return (resid.astype(jnp.float32) + update).astype(jnp.bfloat16)


def solution(mesh):
    group = mesh.shape['cp']
    to_next = [(device_idx, device_idx + 1) for device_idx in range(group - 1)]
    to_prev = [(device_idx + 1, device_idx) for device_idx in range(group - 1)]

    def device_body(hidden, lengths, w_qkv, w_out, w_in, w_mlp_out, attn_gamma, mlp_gamma):
        chunk_len = hidden.shape[1]
        seq_offset = lax.axis_index('cp') * chunk_len
        positions = seq_offset + jnp.arange(chunk_len)
        resid = hidden
        for layer_idx in range(3):
            is_global = LAYER_GLOBAL[layer_idx]
            rope_theta = THETA_GLOBAL if is_global else THETA_LOCAL
            queries, key_val = project_qkv(resid, attn_gamma[layer_idx], w_qkv[layer_idx], positions, rope_theta)
            if is_global:
                key_val_all = lax.all_gather(key_val, 'cp', axis=1, tiled=True)
                attn_out = global_attention(queries, key_val_all, seq_offset, lengths)
            else:
                from_prev = lax.ppermute(key_val[:, chunk_len - WINDOW_HALF:], 'cp', to_next)
                from_next = lax.ppermute(key_val[:, :WINDOW_HALF], 'cp', to_prev)
                key_val_ext = jnp.concatenate([from_prev, key_val, from_next], axis=1)
                attn_out = local_attention(queries, key_val_ext, seq_offset, lengths)
            resid = add_attention(resid, attn_out, w_out[layer_idx])
            resid = mlp_block(resid, mlp_gamma[layer_idx], w_in[layer_idx], w_mlp_out[layer_idx])
        return resid

    act_spec = P('dp', 'cp', None)
    return jax.shard_map(device_body, mesh=mesh, in_specs=(act_spec, P('dp'), P(), P(), P(), P(), P(), P()), out_specs=act_spec, check_vma=False)
```

profile of v0, /device:TPU:0, one launch (start us, length us, event | category | flops | bytes accessed | tf_op | source)
XLA Modules:
  0.0 1859.5 jit_solution(13902889999396837008)
XLA Ops:
  14.3 29.9 %fusion.169 = bf16[3,384,5376]{2,1,0:T(8,128)(2,1)} fusion(bf16[3,1792,5376]{2,1,0:T(8,128)(2,1)} %param.12, bf16[3,384,1792]{2,1,0:T(8,128)(2,1)} %param.10, f32[1792]{0:T(1024)S(1)} %get-tuple-element.69, f32[3,384]{1,0:T(4,128)S(1)} %add_rsqrt_fusion.5, f32[3,384]{1,0:T(4,128)S(1)} %broadcast_multiply_fusion.5), kind=kOutput, calls=%fused_computation.196 | convolution fusion | flops 22212771840 | bytes 35799040 | tf_op jit(solution)/shard_map/bsd,de->bse/dot_general | solution.py:90
  123.8 19.4 %fusion.313 = f32[3,3,28,128,256]{4,3,2,1,0:T(8,128)} fusion(bf16[3,3,256,2,28,64]{2,5,4,1,0,3:T(8,128)(2,1)} %bitcast_dynamic-update-slice_fusion.3, bf16[3,3,128,28,32]{2,4,3,1,0:T(8,128)(2,1)S(1)} %bitcast.266, bf16[3,3,128,28,32]{2,4,3,1,0:T(8,128)(2,1)} %bitcast.267), kind=kOutput, calls=%fused_computation.344 | convolution fusion | flops 1065222144 | bytes 45416448 | tf_op jit(solution)/shard_map/bnqhd,bnkhd->bnhqk/dot_general | solution.py:56
  143.2 43.8 %fusion.493 = (f32[3,3,28,128]{3,2,1,0:T(8,128)S(1)}, f32[3,3,28,128,256]{4,3,2,1,0:T(8,128)}) fusion(f32[3,3,28,128,256]{4,3,2,1,0:T(8,128)} %fusion.313, pred[3,3,128,256]{3,2,1,0:T(8,128)(4,1)S(1)} %broadcast_and_fusion), kind=kOutput, calls=%fused_computation.575 | output fusion | flops 49545472 | bytes 66484224 | tf_op jit(solution)/shard_map/sub | solution.py:38
  243.9 38.1 %fusion.151 = bf16[3,384,7680]{2,1,0:T(8,128)(2,1)} fusion(bf16[3,1792,7680]{2,1,0:T(8,128)(2,1)} %param.14, bf16[3,384,1792]{2,1,0:T(8,128)(2,1)S(1)} %get-tuple-element.131, f32[1792]{0:T(1024)S(1)} %get-tuple-element.66, f32[3,384]{1,0:T(4,128)S(1)} %add_rsqrt_fusion.4, f32[3,384]{1,0:T(4,128)S(1)} %broadcast_multiply_fusion.4), kind=kOutput, calls=%fused_computation.166 | convolution fusion | flops 31728107520 | bytes 49364992 | tf_op jit(solution)/shard_map/bsd,de->bse/dot_general | solution.py:103
  282.0 61.8 %convert_reduce_fusion.3 = (f32[3,384]{1,0:T(4,128)S(1)}, bf16[3,384,1792]{2,1,0:T(8,128)(2,1)S(1)}) fusion(bf16[3,3840,1792]{2,1,0:T(8,128)(2,1)} %param.15, bf16[3,384,7680]{2,1,0:T(8,128)(2,1)} %fusion.151, bf16[3,384,1792]{2,1,0:T(8,128)(2,1)} %copy-done.8), kind=kOutput, calls=%fused_computation.189 | convolution fusion | flops 16165600256 | bytes 39719424 | tf_op jit(solution)/shard_map/bsf,fd->bsd/dot_general | solution.py:106
  345.8 28.9 %fusion.172 = bf16[3,384,5376]{2,1,0:T(8,128)(2,1)} fusion(bf16[3,1792,5376]{2,1,0:T(8,128)(2,1)} %param.12, bf16[3,384,1792]{2,1,0:T(8,128)(2,1)S(1)} %get-tuple-element.133, f32[1792]{0:T(1024)S(1)} %copy-done.25, f32[3,384]{1,0:T(4,128)S(1)} %add_rsqrt_fusion.3, f32[3,384]{1,0:T(4,128)S(1)} %broadcast_multiply_fusion.3), kind=kOutput, calls=%fused_computation.197 | convolution fusion | flops 22212771840 | bytes 35799040 | tf_op jit(solution)/shard_map/bsd,de->bse/dot_general | solution.py:90
  402.8 28.1 %collective-permute-start.2 = (bf16[3,64,2,28,64]{1,4,3,0,2:T(8,128)(2,1)S(1)}, bf16[3,64,2,28,64]{1,4,3,0,2:T(8,128)(2,1)S(1)}, u32[]{:S(2)}, u32[]{:S(2)}) collective-permute-start(bf16[3,64,2,28,64]{1,4,3,0,2:T(8,128)(2,1)S(1)} %get-tuple-element.111), channel_id=1, source_target_pairs={{0,1},{1,2},{2,3},{3,4},{4,5},{5,6},{6,7},{8,9},{9,10},{10,11},{11... | collective-permute-start | bytes 4128776 | tf_op jit(solution)/shard_map/ppermute | solution.py:128
  469.9 19.4 %fusion.310 = f32[3,3,28,128,256]{4,3,2,1,0:T(8,128)} fusion(bf16[3,3,256,2,28,64]{2,5,4,1,0,3:T(8,128)(2,1)} %bitcast_dynamic-update-slice_fusion.1, bf16[3,3,128,28,32]{2,4,3,1,0:T(8,128)(2,1)S(1)} %bitcast.268, bf16[3,3,128,28,32]{2,4,3,1,0:T(8,128)(2,1)} %bitcast.269), kind=kOutput, calls=%fused_computation.333 | convolution fusion | flops 1065222144 | bytes 45416448 | tf_op jit(solution)/shard_map/bnqhd,bnkhd->bnhqk/dot_general | solution.py:56
  489.3 33.5 %fusion.494 = (f32[3,3,28,128]{3,2,1,0:T(8,128)S(1)}, f32[3,3,28,128,256]{4,3,2,1,0:T(8,128)}) fusion(f32[3,3,28,128,256]{4,3,2,1,0:T(8,128)} %fusion.310, pred[3,3,128,256]{3,2,1,0:T(8,128)(4,1)S(1)} %copy-done.15), kind=kOutput, calls=%fused_computation.576 | output fusion | flops 49545472 | bytes 66484224 | tf_op jit(solution)/shard_map/sub | solution.py:38
  522.8 17.3 fusion.339
  579.7 38.1 %fusion.154 = bf16[3,384,7680]{2,1,0:T(8,128)(2,1)} fusion(bf16[3,1792,7680]{2,1,0:T(8,128)(2,1)} %param.14, bf16[3,384,1792]{2,1,0:T(8,128)(2,1)S(1)} %get-tuple-element.137, f32[1792]{0:T(1024)S(1)} %copy-done.24, f32[3,384]{1,0:T(4,128)S(1)} %add_rsqrt_fusion.2, f32[3,384]{1,0:T(4,128)S(1)} %broadcast_multiply_fusion.2), kind=kOutput, calls=%fused_computation.167 | convolution fusion | flops 31728107520 | bytes 49364992 | tf_op jit(solution)/shard_map/bsd,de->bse/dot_general | solution.py:103
  617.8 61.8 %convert_reduce_fusion.1 = (f32[3,384]{1,0:T(4,128)S(1)}, bf16[3,384,1792]{2,1,0:T(8,128)(2,1)S(1)}) fusion(bf16[3,3840,1792]{2,1,0:T(8,128)(2,1)} %param.15, bf16[3,384,7680]{2,1,0:T(8,128)(2,1)} %fusion.154, bf16[3,384,1792]{2,1,0:T(8,128)(2,1)} %copy-done.7), kind=kOutput, calls=%fused_computation.183 | convolution fusion | flops 16165600256 | bytes 39719424 | tf_op jit(solution)/shard_map/bsf,fd->bsd/dot_general | solution.py:106
  681.5 28.9 %fusion.175 = bf16[3,384,5376]{2,1,0:T(8,128)(2,1)} fusion(bf16[3,1792,5376]{2,1,0:T(8,128)(2,1)} %param.12, bf16[3,384,1792]{2,1,0:T(8,128)(2,1)S(1)} %get-tuple-element.139, f32[1792]{0:T(1024)S(1)} %copy-done.23, f32[3,384]{1,0:T(4,128)S(1)} %add_rsqrt_fusion.1, f32[3,384]{1,0:T(4,128)S(1)} %broadcast_multiply_fusion.1), kind=kOutput, calls=%fused_computation.198 | convolution fusion | flops 22212771840 | bytes 35799040 | tf_op jit(solution)/shard_map/bsd,de->bse/dot_general | solution.py:90
  760.0 563.4 %all-gather.2.cloned.1.call-done = bf16[3,3072,2,28,64]{1,4,3,2,0:T(8,128)(2,1)} async-done(((bf16[3,384,2,28,64]{1,4,3,2,0:T(8,128)(2,1)}), bf16[3,3072,2,28,64]{1,4,3,2,0:T(8,128)(2,1)}) %all-gather.2.cloned.1.call-update) | async-done | bytes 66060304 | tf_op jit(solution)/shard_map/all_gather | solution.py:125
  1323.4 44.1 %slice_bitcast_fusion = (bf16[3,3072,28,64]{1,3,2,0:T(8,128)(2,1)}, bf16[3,3072,28,64]{1,3,2,0:T(8,128)(2,1)}) fusion(bf16[3,3072,2,28,64]{1,4,3,2,0:T(8,128)(2,1)} %all-gather.2.cloned.1.call-done), kind=kLoop, calls=%fused_computation.25 | loop fusion | bytes 132120576 | tf_op jit(solution)/shard_map/squeeze | solution.py:74
  1367.5 342.3 %while.11 = (s32[]{:T(128)}, bf16[3,3,128,28,64]{2,4,3,1,0:T(8,128)(2,1)}, bf16[3,3,128,28,64]{2,4,3,1,0:T(8,128)(2,1)}, bf16[3,3072,28,64]{1,3,2,0:T(8,128)(2,1...) while((s32[]{:T(128)}, ...), condition=%wide.region_17.18_spmd.clone, body=%wide.region_14.17_spmd.clone.sunk | while | flops 8653910016 | bytes 334535840 | solution.py:82
  1367.6 60.5 %fusion.515 = (f32[3,28,128]{2,1,0:T(8,128)S(1)}, f32[3,28,128,3072]{3,2,1,0:T(8,128)}) fusion(pred[3,3072]{1,0:T(4,128)(4,1)S(1)} %fusion.514, bf16[3,3072,28,64]{1,3,2,0:T(8,128)(2,1)} %get-tuple-element.202, bf16[3,3,128,28,64]{2,4,3,1,0:T(8,128)(2,1)} %get-tuple-element.201, s32[]{:T(128)} %get-tuple-element.192), kind=kOutput, calls=%fused_computation.574.clone.1 | convolution fusion | flops 4359982080 | bytes 166579712 | tf_op jit(solution)/shard_map/while/body/eval_jaxpr/sub | solution.py:38
  1428.0 53.5 %bitcast_dynamic-update-slice_fusion.6 = bf16[3,3,128,28,64]{2,4,3,1,0:T(8,128)(2,1)} fusion(bf16[3,3,128,28,64]{2,4,3,1,0:T(8,128)(2,1)} %get-tuple-element.193, s32[]{:T(128)} %get-tuple-element.192, bf16[3,3072,28,64]{1,3,2,0:T(8,128)(2,1)} %get-tuple-element.203, f32[3,28,128,3072]{3,2,1,0:T(8,128)} %get-tuple-element.183, ...), kind=kOutput, calls=%fused_computation.11.clone.1 | convolution fusion | flops 4293918720 | bytes 167946752 | tf_op jit(solution)/shard_map/while/body/eval_jaxpr/bhqk,bkhd->bqhd/dot_general | solution.py:80
  1481.6 60.5 %fusion.515 = (f32[3,28,128]{2,1,0:T(8,128)S(1)}, f32[3,28,128,3072]{3,2,1,0:T(8,128)}) fusion(pred[3,3072]{1,0:T(4,128)(4,1)S(1)} %fusion.514, bf16[3,3072,28,64]{1,3,2,0:T(8,128)(2,1)} %get-tuple-element.202, bf16[3,3,128,28,64]{2,4,3,1,0:T(8,128)(2,1)} %get-tuple-element.201, s32[]{:T(128)} %get-tuple-element.192), kind=kOutput, calls=%fused_computation.574.clone.1 | convolution fusion | flops 4359982080 | bytes 166579712 | tf_op jit(solution)/shard_map/while/body/eval_jaxpr/sub | solution.py:38
  1542.1 53.5 %bitcast_dynamic-update-slice_fusion.6 = bf16[3,3,128,28,64]{2,4,3,1,0:T(8,128)(2,1)} fusion(bf16[3,3,128,28,64]{2,4,3,1,0:T(8,128)(2,1)} %get-tuple-element.193, s32[]{:T(128)} %get-tuple-element.192, bf16[3,3072,28,64]{1,3,2,0:T(8,128)(2,1)} %get-tuple-element.203, f32[3,28,128,3072]{3,2,1,0:T(8,128)} %get-tuple-element.183, ...), kind=kOutput, calls=%fused_computation.11.clone.1 | convolution fusion | flops 4293918720 | bytes 167946752 | tf_op jit(solution)/shard_map/while/body/eval_jaxpr/bhqk,bkhd->bqhd/dot_general | solution.py:80
  1595.6 60.5 %fusion.515 = (f32[3,28,128]{2,1,0:T(8,128)S(1)}, f32[3,28,128,3072]{3,2,1,0:T(8,128)}) fusion(pred[3,3072]{1,0:T(4,128)(4,1)S(1)} %fusion.514, bf16[3,3072,28,64]{1,3,2,0:T(8,128)(2,1)} %get-tuple-element.202, bf16[3,3,128,28,64]{2,4,3,1,0:T(8,128)(2,1)} %get-tuple-element.201, s32[]{:T(128)} %get-tuple-element.192), kind=kOutput, calls=%fused_computation.574.clone.1 | convolution fusion | flops 4359982080 | bytes 166579712 | tf_op jit(solution)/shard_map/while/body/eval_jaxpr/sub | solution.py:38
  1656.1 53.5 %bitcast_dynamic-update-slice_fusion.6 = bf16[3,3,128,28,64]{2,4,3,1,0:T(8,128)(2,1)} fusion(bf16[3,3,128,28,64]{2,4,3,1,0:T(8,128)(2,1)} %get-tuple-element.193, s32[]{:T(128)} %get-tuple-element.192, bf16[3,3072,28,64]{1,3,2,0:T(8,128)(2,1)} %get-tuple-element.203, f32[3,28,128,3072]{3,2,1,0:T(8,128)} %get-tuple-element.183, ...), kind=kOutput, calls=%fused_computation.11.clone.1 | convolution fusion | flops 4293918720 | bytes 167946752 | tf_op jit(solution)/shard_map/while/body/eval_jaxpr/bhqk,bkhd->bqhd/dot_general | solution.py:80
  1750.8 38.1 %fusion.157 = bf16[3,384,7680]{2,1,0:T(8,128)(2,1)} fusion(bf16[3,1792,7680]{2,1,0:T(8,128)(2,1)} %param.14, bf16[3,384,1792]{2,1,0:T(8,128)(2,1)S(1)} %get-tuple-element.141, f32[1792]{0:T(1024)S(1)} %copy-done.22, f32[3,384]{1,0:T(4,128)S(1)} %add_rsqrt_fusion, f32[3,384]{1,0:T(4,128)S(1)} %broadcast_multiply_fusion), kind=kOutput, calls=%fused_computation.168 | convolution fusion | flops 31728107520 | bytes 49364992 | tf_op jit(solution)/shard_map/bsd,de->bse/dot_general | solution.py:103
  1789.0 63.3 %fusion.309 = bf16[3,384,1792]{2,1,0:T(8,128)(2,1)} fusion(bf16[3,384,1792]{2,1,0:T(8,128)(2,1)} %copy-done.9, bf16[3,3840,1792]{2,1,0:T(8,128)(2,1)} %param.15, bf16[3,384,7680]{2,1,0:T(8,128)(2,1)} %fusion.157), kind=kOutput, calls=%fused_computation.327 | convolution fusion | flops 16161472512 | bytes 39714816 | tf_op jit(solution)/shard_map/bsf,fd->bsd/dot_general | solution.py:106
  (148 shorter events, 345.4 us)
Async XLA Ops:
  6.5 1316.8 %all-gather.2.cloned.1.call-start = ((), (), s32[]{:S(2)}) async-start(), calls=%async_computation | async-start | bytes 74317824 | tf_op jit(solution)/shard_map/all_gather | solution.py:125
  71.6 9.2 copy-start.21
  71.6 16.6 copy-start.18
  75.2 13.4 collective-permute-start
  79.2 9.4 collective-permute-start.1
  88.3 98.8 %copy-start.27 = (pred[3,3,128]{2,1,0:T(4,128)(4,1)}, pred[3,3,128]{2,1,0:T(4,128)(4,1)S(1)}, u32[]{:S(2)}) copy-start(pred[3,3,128]{2,1,0:T(4,128)(4,1)S(1)} %broadcast_compare_fusion) | copy-start | bytes 3460
  88.6 54.5 %copy-start.14 = (pred[3,3,128,256]{3,2,1,0:T(8,128)(4,1)}, pred[3,3,128,256]{3,2,1,0:T(8,128)(4,1)S(1)}, u32[]{:S(2)}) copy-start(pred[3,3,128,256]{3,2,1,0:T(8,128)(4,1)S(1)} %broadcast_and_fusion) | copy-start | bytes 884740
  114.5 9.3 copy-start.2
  282.0 63.8 %copy-start.25 = (f32[1792]{0:T(1024)S(1)}, f32[1792]{0:T(1024)}, u32[]{:S(2)}) copy-start(f32[1792]{0:T(1024)} %get-tuple-element.70) | copy-start | bytes 21508
  400.7 31.5 %copy-start.4 = (bf16[3,28,4,3,8,128]{5,4,3,2,1,0:T(8,128)(2,1)S(1)}, bf16[3,28,4,3,8,128]{5,4,3,2,1,0:T(8,128)(2,1)}, u32[]{:S(2)}) copy-start(bf16[3,28,4,3,8,128]{5,4,3,2,1,0:T(8,128)(2,1)} %get-tuple-element.101) | copy-start | bytes 6193156
  400.7 31.9 %copy-start.3 = (bf16[3,28,4,3,8,128]{5,4,3,2,1,0:T(8,128)(2,1)S(1)}, bf16[3,28,4,3,8,128]{5,4,3,2,1,0:T(8,128)(2,1)}, u32[]{:S(2)}) copy-start(bf16[3,28,4,3,8,128]{5,4,3,2,1,0:T(8,128)(2,1)} %get-tuple-element.100) | copy-start | bytes 6193156
  402.8 32.6 %collective-permute-start.2 = (bf16[3,64,2,28,64]{1,4,3,0,2:T(8,128)(2,1)S(1)}, bf16[3,64,2,28,64]{1,4,3,0,2:T(8,128)(2,1)S(1)}, u32[]{:S(2)}, u32[]{:S(2)}) collective-permute-start(bf16[3,64,2,28,64]{1,4,3,0,2:T(8,128)(2,1)S(1)} %get-tuple-element.111), channel_id=1, source_target_pairs={{0,1},{1,2},{2,3},{3,4},{4,5},{5,6},{6,7},{8,9},{9,10},{10,11},{11... | collective-permute-start | bytes 4128776 | tf_op jit(solution)/shard_map/ppermute | solution.py:128
  430.9 7.0 collective-permute-start.3
  469.9 19.4 %copy-start.15 = (pred[3,3,128,256]{3,2,1,0:T(8,128)(4,1)S(1)}, pred[3,3,128,256]{3,2,1,0:T(8,128)(4,1)}, u32[]{:S(2)}) copy-start(pred[3,3,128,256]{3,2,1,0:T(8,128)(4,1)} %copy-done.14) | copy-start | bytes 884740
  489.3 33.5 %copy-start.28 = (pred[3,3,128]{2,1,0:T(4,128)(4,1)S(1)}, pred[3,3,128]{2,1,0:T(4,128)(4,1)}, u32[]{:S(2)}) copy-start(pred[3,3,128]{2,1,0:T(4,128)(4,1)} %copy-done.27) | copy-start | bytes 3460
  564.3 15.4 copy-start.24
  617.8 63.7 %copy-start.23 = (f32[1792]{0:T(1024)S(1)}, f32[1792]{0:T(1024)}, u32[]{:S(2)}) copy-start(f32[1792]{0:T(1024)} %get-tuple-element.68) | copy-start | bytes 21508
  727.0 5.7 copy-start.17
  760.0 607.5 %copy-start.19 = (s32[3]{0:T(128)S(1)}, s32[3]{0:T(128)}, u32[]{:S(2)}) copy-start(s32[3]{0:T(128)} %param.11) | copy-start | bytes 40
  1367.4 342.3 %copy-start.26 = (pred[3,3,128]{2,0,1:T(4,128)(4,1)S(1)}, pred[3,3,128]{2,0,1:T(4,128)(4,1)}, u32[]{:S(2)}) copy-start(pred[3,3,128]{2,0,1:T(4,128)(4,1)} %copy.46) | copy-start | bytes 3460
  1428.0 53.5 %copy-start.20 = (s32[3]{0:T(128)S(1)}, s32[3]{0:T(128)}, u32[]{:S(2)}) copy-start(s32[3]{0:T(128)} %get-tuple-element.221) | copy-start | bytes 40 | tf_op jit(solution)/shard_map/while
  1542.1 53.5 %copy-start.20 = (s32[3]{0:T(128)S(1)}, s32[3]{0:T(128)}, u32[]{:S(2)}) copy-start(s32[3]{0:T(128)} %get-tuple-element.221) | copy-start | bytes 40 | tf_op jit(solution)/shard_map/while
  1656.1 53.5 %copy-start.20 = (s32[3]{0:T(128)S(1)}, s32[3]{0:T(128)}, u32[]{:S(2)}) copy-start(s32[3]{0:T(128)} %get-tuple-element.221) | copy-start | bytes 40 | tf_op jit(solution)/shard_map/while
  1735.4 15.4 copy-start.22
  (13 other events, 47.5 us)
Sparse Core Ops, SparseCore 0:
  740.3 583.0 all-gather.1
where the time goes:
time: 1870 us; the launch traced here: 1860 us
  matrix products  844 us (45%)
  waiting for transfers between devices  567 us (30%)
  local copies, waits for them, and re-layouts  229 us (12%)
  other arithmetic  170 us (9%)
  starting transfers between devices  34.9 us (2%)
    all_gather x1, waiting for transfers between devices, device_body(): key_val_all = lax.all_gather(key_val, 'cp', axis=1, tiled=True)  563 us
    dot_general x3, matrix products, mlp_block(): jnp.einsum('bsf,fd->bsd', gated_act, w_mlp_out_layer, preferred_element_t...  187 us
    sub x3, matrix products, masked_softmax(): exp_scores = jnp.exp(scores - row_max)  181 us
    dot_general x3, matrix products, one_block(): jnp.einsum('bhqk,bkhd->bqhd', attn_probs, values_all, preferred_element_t...  160 us
    dot_general x3, matrix products, mlp_block(): jnp.einsum('bsd,de->bse', normed, w_in_layer, preferred_element_type=jnp....  114 us
    dot_general x3, matrix products, project_qkv(): jnp.einsum('bsd,de->bse', normed, w_qkv_layer, preferred_element_type=jnp...  87.8 us
    sub x2, other arithmetic, masked_softmax(): exp_scores = jnp.exp(scores - row_max)  77.4 us
    convert_element_type x6, local copies, waits for them, and re-layouts, finish_rows(): return jnp.where(row_ok, attn_out, 0.0).astype(jnp.bfloat16)  70.6 us
  transfers between devices with their start and end apart: 5, of which 3 were waited for; matrix products, arithmetic and copies ran while one was open for 2% of the time, Pallas kernels for 0%

commit v1 on v0

v1 whole, which is shorter than its diff:
```python
import functools

import jax
import jax.numpy as jnp
from jax import lax
from jax.experimental import pallas as pl
from jax.experimental.pallas import tpu as pltpu
from jax.sharding import PartitionSpec as P


D = 1792
FF = 3840
HEAD_DIM = 64
HALO = 64
ROWS = 384
SEQ = 3072
GROUP = 8
OWNERS = 7
WIDE = 256
N_HEADS_WIDE = D // WIDE
T_OUT = 896
N_OUT = D // T_OUT
TILE = 768
N_QKV = 3 * D // TILE
N_MLP = FF // TILE
GQ = 1024
GK = 1024
VMEM_LIMIT = 66 * 1000 * 1000
THETA_LOCAL = 10000.0
THETA_GLOBAL = 160000.0
LN_EPS = 1e-5
NEG = -1e30
F32 = jnp.float32
BF16 = jnp.bfloat16


def dot(a, b):
    return lax.dot_general(a, b, (((1,), (0,)), ((), ())), preferred_element_type=F32)


def rope_tables(positions, theta):
    inv_freq = theta ** (-jnp.arange(0, HEAD_DIM, 2, dtype=F32) / HEAD_DIM)
    angles = positions.astype(F32)[:, None] * inv_freq[None, :]
    cos, sin = jnp.cos(angles), jnp.sin(angles)
    return jnp.concatenate([cos] * 4, axis=1), jnp.concatenate([-sin, sin, -sin, sin], axis=1)


def rotate(y, cos, sin):
    y = y.astype(BF16).astype(F32)
    lane = lax.broadcasted_iota(jnp.int32, (1, 128), 1)
    low = lane % HEAD_DIM < HEAD_DIM // 2
    parts = []
    for c in range(y.shape[1] // 128):
        part = y[:, c * 128:(c + 1) * 128]
        other = jnp.where(low, pltpu.roll(part, 96, 1), pltpu.roll(part, 32, 1))
        parts.append(part * cos + other * sin)
    return jnp.concatenate(parts, axis=1).astype(BF16)


def norm_rows(src, gamma, dst, n_rows, step=16):
    def one(r, carry):
        rows = pl.ds(pl.multiple_of(r * step, step), step)
        x = src[rows, :].astype(BF16).astype(F32)
        mean = jnp.sum(x, axis=1, keepdims=True) * (1.0 / D)
        c = x - mean
        var = jnp.sum(c * c, axis=1, keepdims=True) * (1.0 / D)
        dst[rows, :] = (c * lax.rsqrt(var + LN_EPS) * gamma).astype(BF16)
        return carry

    lax.fori_loop(0, n_rows // step, one, 0, unroll=2)


def gelu_gate(u):
    a = u[:, :TILE].astype(F32)
    g = u[:, TILE:].astype(F32)
    return (a * (0.5 * (1.0 + lax.erf(a * (2.0 ** -0.5)))) * g).astype(BF16)


def rope_pass(out, groups, cos, sin, step=32):
    def one(r, carry):
        src = pl.ds(pl.multiple_of(r * step, step), step)
        c, s = cos[src, :], sin[src, :]
        for doc in range(out.shape[0] // ROWS):
            rows = pl.ds(pl.multiple_of(doc * ROWS + r * step, step), step)
            for g in range(groups):
                cols = slice(g * 128, (g + 1) * 128)
                out[rows, cols] = rotate(out[rows, cols], c, s)
        return carry

    lax.fori_loop(0, ROWS // step, one, 0)


def qkv_tile(t, h, w_qkv, cos, sin, qkv):
    qkv[...] = dot(h[...], w_qkv).astype(BF16)
    whole_tiles, rest = divmod(2 * D, TILE)

    @pl.when(t < whole_tiles)
    def _():
        rope_pass(qkv, TILE // 128, cos, sin)

    @pl.when(t == whole_tiles)
    def _():
        rope_pass(qkv, rest // 128, cos, sin)


def first_kernel(layer, after, x, w_qkv, gamma, cos, sin, qkv, h):
    t = pl.program_id(0)

    @pl.when(t == 0)
    def _():
        norm_rows(x, gamma[layer:layer + 1, :], h, x.shape[0])

    qkv_tile(t, h, w_qkv[...], cos, sin, qkv)


def whole(shape):
    return pl.BlockSpec(shape, lambda *_: (0,) * len(shape), pipeline_mode=pl.Buffered(1))


def cost(flops, nbytes):
    return pl.CostEstimate(flops=int(flops * 0.01), bytes_accessed=int(nbytes), transcendentals=0)


def first_block(after, x, w_qkv, gamma, cos, sin, layer):
    n_rows = x.shape[0]
    return pl.pallas_call(
        functools.partial(first_kernel, layer),
        grid=(N_QKV,),
        in_specs=[pl.BlockSpec(memory_space=pl.ANY), whole((n_rows, D)), pl.BlockSpec((None, D, TILE), lambda i: (layer, 0, i)), whole((3, D)), whole((ROWS, 128)), whole((ROWS, 128))],
        out_specs=pl.BlockSpec((n_rows, TILE), lambda i: (0, i)),
        out_shape=jax.ShapeDtypeStruct((n_rows, 3 * D), BF16),
        scratch_shapes=[pltpu.VMEM((n_rows, D), BF16)],
        cost_estimate=cost(2 * n_rows * D * 3 * D, 2 * D * 3 * D),
        compiler_params=pltpu.CompilerParams(vmem_limit_bytes=VMEM_LIMIT),
        name="first_qkv",
    )(after, x, w_qkv, gamma, cos, sin)


def post_kernel(layer, mode, n_o, *refs):
    refs = list(refs)
    where, _ = refs.pop(0), refs.pop(0)
    o_refs = [refs.pop(0) for _ in range(n_o)]
    x, w_out, w_in, w_mlp_out, mlp_gamma = [refs.pop(0) for _ in range(5)]
    if mode == "qkv":
        w_qkv, attn_gamma, cos, sin = [refs.pop(0) for _ in range(4)]
        x_out, qkv = refs.pop(0), refs.pop(0)
    elif mode == "norm":
        attn_gamma = refs.pop(0)
        x_out, h_out = refs.pop(0), refs.pop(0)
    else:
        x_out = refs.pop(0)
    h, acc, u_even, u_odd, wo, wa, wg, wd, sem_o, sem_a, sem_g, sem_d = [refs.pop(0) for _ in range(12)]
    if mode == "qkv":
        wq, sem_q = refs.pop(0), refs.pop(0)
    o_full = refs.pop(0) if n_o > 1 else o_refs[0]
    n_rows = x.shape[0]
    i = pl.program_id(0)
    j = i - N_OUT

    def tile(t):
        return pl.ds(pl.multiple_of(t * TILE, 128), TILE)

    def out_copy(c):
        cols = pl.ds(pl.multiple_of(c * T_OUT, 128), T_OUT)
        return pltpu.make_async_copy(w_out.at[layer, :, cols], wo.at[c], sem_o.at[c])

    def up_copies(t):
        slot = lax.rem(t, 2)
        gate = pl.ds(pl.multiple_of(FF + t * TILE, 128), TILE)
        return (
            pltpu.make_async_copy(w_in.at[layer, :, tile(t)], wa.at[slot], sem_a.at[slot]),
            pltpu.make_async_copy(w_in.at[layer, :, gate], wg.at[slot], sem_g.at[slot]),
        )

    def down_copy(t):
        slot = lax.rem(t, 2)
        return pltpu.make_async_copy(w_mlp_out.at[layer, tile(t), :], wd.at[slot], sem_d.at[slot])

    def qkv_copy(t):
        slot = lax.rem(t, 2)
        return pltpu.make_async_copy(w_qkv.at[layer + 1, :, tile(t)], wq.at[slot], sem_q.at[slot])

    @pl.when(i == 0)
    def _():
        for c in range(N_OUT):
            out_copy(jnp.int32(c)).start()
        for c in up_copies(jnp.int32(0)):
            c.start()
        down_copy(jnp.int32(0)).start()
        if n_o > 1:
            for k in range(n_o):
                source = lax.rem(where[0] - k + n_o, n_o)

                @pl.when(source < OWNERS)
                def _():
                    o_full[:, pl.ds(pl.multiple_of(source * WIDE, WIDE), WIDE)] = o_refs[k][...]

    @pl.when(i < N_OUT)
    def _():
        out_copy(i).wait()
        cols = pl.ds(pl.multiple_of(i * T_OUT, 128), T_OUT)
        acc[:, cols] = (x[:, cols].astype(F32) + dot(o_full[...], wo[i])).astype(BF16).astype(F32)

    @pl.when(j == 0)
    def _():
        norm_rows(acc, mlp_gamma[layer:layer + 1, :], h, n_rows)

    @pl.when((j >= 0) & (j < N_MLP - 1))
    def _():
        for c in up_copies(j + 1):
            c.start()

    @pl.when((j >= 1) & (j < N_MLP))
    def _():
        down_copy(j).start()

    @pl.when((j >= 0) & (j < N_MLP))
    def _():
        for c in up_copies(j):
            c.wait()

    @pl.when((j >= 1) & (j <= N_MLP))
    def _():
        down_copy(j - 1).wait()

    if mode == "qkv":
        @pl.when((j >= N_MLP - 1) & (j <= N_MLP))
        def _():
            qkv_copy(j - N_MLP + 1).start()

    slot = lax.rem(jnp.maximum(j, 0), 2)

    def project(u):
        u[:, :TILE] = dot(h[...], wa[slot]).astype(BF16)
        u[:, TILE:] = dot(h[...], wg[slot]).astype(BF16)

    def consume(u):
        acc[...] += dot(gelu_gate(u[...]), wd[1 - slot])

    @pl.when(j == 0)
    def _():
        project(u_even)

    @pl.when((j > 0) & (j < N_MLP) & (slot == 1))
    def _():
        consume(u_even)
        project(u_odd)

    @pl.when((j > 0) & (j < N_MLP) & (slot == 0))
    def _():
        consume(u_odd)
        project(u_even)

    @pl.when(j == N_MLP)
    def _():
        consume(u_even if (N_MLP - 1) % 2 == 0 else u_odd)
        x_out[...] = acc[...].astype(BF16)
        if mode == "qkv":
            norm_rows(acc, attn_gamma[layer + 1:layer + 2, :], h, n_rows)
        elif mode == "norm":
            norm_rows(acc, attn_gamma[layer + 1:layer + 2, :], h_out, n_rows)

    if mode == "qkv":
        t = j - N_MLP - 1

        @pl.when(t >= 0)
        def _():
            qkv_copy(t).wait()
            qkv_tile(t, h, wq[lax.rem(t, 2)], cos, sin, qkv)

        @pl.when((t >= 0) & (t < N_QKV - 2))
        def _():
            qkv_copy(t + 2).start()


def post_block(after, where, o_parts, x, weights, layer, mode, cos=None, sin=None):
    w_qkv, w_out, w_in, w_mlp_out, attn_gamma, mlp_gamma = weights
    n_o = len(o_parts)
    n_rows = x.shape[0]
    base = N_OUT + N_MLP + 1
    steps = base + (N_QKV if mode == "qkv" else 0)
    hbm = pl.BlockSpec(memory_space=pl.ANY)
    full = whole((n_rows, D))
    in_specs = [hbm] + [whole(o.shape) for o in o_parts] + [full, hbm, hbm, hbm, whole((3, D))]
    args = [after] + list(o_parts) + [x, w_out, w_in, w_mlp_out, mlp_gamma]
    out_specs = [full]
    out_shape = [jax.ShapeDtypeStruct((n_rows, D), BF16)]
    flops = 2 * n_rows * D * (D + 3 * FF)
    sem = pltpu.SemaphoreType.DMA((2,))
    scratch = [
        pltpu.VMEM((n_rows, D), BF16),
        pltpu.VMEM((n_rows, D), F32),
        pltpu.VMEM((n_rows, 2 * TILE), BF16),
        pltpu.VMEM((n_rows, 2 * TILE), BF16),
        pltpu.VMEM((2, D, T_OUT), BF16),
        pltpu.VMEM((2, D, TILE), BF16),
        pltpu.VMEM((2, D, TILE), BF16),
        pltpu.VMEM((2, TILE, D), BF16),
        sem, sem, sem, sem,
    ]
    if mode == "qkv":
        in_specs += [hbm, whole((3, D)), whole((ROWS, 128)), whole((ROWS, 128))]
        args += [w_qkv, attn_gamma, cos, sin]
        out_specs.append(pl.BlockSpec((n_rows, TILE), lambda i, *_: (0, jnp.clip(i - base, 0, N_QKV - 1))))
        out_shape.append(jax.ShapeDtypeStruct((n_rows, 3 * D), BF16))
        flops += 2 * n_rows * D * 3 * D
        scratch += [pltpu.VMEM((2, D, TILE), BF16), sem]
    elif mode == "norm":
        in_specs.append(whole((3, D)))
        args.append(attn_gamma)
        out_specs.append(full)
        out_shape.append(jax.ShapeDtypeStruct((n_rows, D), BF16))
    if n_o > 1:
        scratch.append(pltpu.VMEM((n_rows, D), BF16))
    return pl.pallas_call(
        functools.partial(post_kernel, layer, mode, n_o),
        grid_spec=pltpu.PrefetchScalarGridSpec(
            num_scalar_prefetch=1, grid=(steps,), in_specs=in_specs, out_specs=out_specs, scratch_shapes=scratch
        ),
        out_shape=out_shape,
        cost_estimate=cost(flops, flops / n_rows),
        compiler_params=pltpu.CompilerParams(vmem_limit_bytes=VMEM_LIMIT),
    )(where, *args)


def local_kernel(where, after, q, k, v, pk, pv, nk, nv, out, bias):
    offset, length = where[0], where[1 + pl.program_id(0)]

    @pl.when(pl.program_id(1) == 0)
    def _():
        row = lax.broadcasted_iota(jnp.int32, (256, 256), 0) % 128
        col = lax.broadcasted_iota(jnp.int32, (256, 256), 1)
        window = (col >= row) & (col <= row + 2 * HALO)
        for b in range(ROWS // 128):
            pos = offset - HALO + b * 128 + col
            bias[b] = jnp.where(window & (pos >= 0) & (pos < length), 0.0, NEG)

    low = lax.broadcasted_iota(jnp.int32, (1, 128), 1) < HEAD_DIM
    for pair in range(WIDE // 128):
        cols = slice(pair * 128, (pair + 1) * 128)
        k_t = jnp.concatenate([pk[:, cols], k[:, cols], nk[:, cols]], axis=0).T
        v_ext = jnp.concatenate([pv[:, cols], v[:, cols], nv[:, cols]], axis=0)
        n_blocks = ROWS // 128
        rows = [slice(b * 128, (b + 1) * 128) for b in range(n_blocks)]
        spans = [slice(b * 128, b * 128 + 256) for b in range(n_blocks)]
        scores = []
        for b in range(n_blocks):
            qs = q[rows[b], cols] * jnp.asarray(HEAD_DIM ** -0.5, BF16)
            zero = jnp.zeros_like(qs)
            both = jnp.concatenate([jnp.where(low, qs, zero), jnp.where(low, zero, qs)], axis=0)
            scores.append(dot(both, k_t[:, spans[b]]) + bias[b])
        exps = [jnp.exp(s - jnp.max(s, axis=1, keepdims=True)) for s in scores]
        sums = [jnp.sum(e, axis=1, keepdims=True) for e in exps]
        for b in range(n_blocks):
            o = dot(exps[b].astype(BF16), v_ext[spans[b]]) * (1.0 / sums[b])
            ok = offset + b * 128 + lax.broadcasted_iota(jnp.int32, (128, 1), 0) < length
            out[rows[b], cols] = jnp.where(ok, jnp.where(low, o[:128], o[128:]), 0.0).astype(BF16)


def local_block(after, where, qkv, prev, nxt):
    n_rows = qkv.shape[0]

    def main(part):
        return pl.BlockSpec((ROWS, WIDE), lambda d, i, *_: (d, part * N_HEADS_WIDE + i))

    def edge(part):
        return pl.BlockSpec((HALO, WIDE), lambda d, i, *_: (d, part * N_HEADS_WIDE + i))

    return pl.pallas_call(
        local_kernel,
        grid_spec=pltpu.PrefetchScalarGridSpec(
            num_scalar_prefetch=1,
            grid=(n_rows // ROWS, N_HEADS_WIDE),
            in_specs=[pl.BlockSpec(memory_space=pl.ANY), main(0), main(1), main(2), edge(0), edge(1), edge(0), edge(1)],
            out_specs=main(0),
            scratch_shapes=[pltpu.VMEM((ROWS // 128, 256, 256), F32)],
        ),
        out_shape=jax.ShapeDtypeStruct((n_rows, D), BF16),
        cost_estimate=cost(15e6 * n_rows, 6 * n_rows * D),
        name="local_attn",
    )(where, after, qkv, qkv, qkv, prev, prev, nxt, nxt)


def project_kernel(where, after, h, wq, wk, wv, cos, sin, q, k_t, v):
    @pl.when(pl.program_id(0) * 512 < where[1])
    def _():
        hv = h[...]
        q[...] = rotate(dot(hv, wq[...]), cos[...], sin[...]) * jnp.asarray(HEAD_DIM ** -0.5, BF16)
        k_t[...] = rotate(dot(hv, wk[...]), cos[...], sin[...]).T
        v[...] = dot(hv, wv[...]).astype(BF16)

    @pl.when(pl.program_id(0) * 512 >= where[1])
    def _():
        for ref in (q, k_t, v):
            ref[...] = jnp.zeros_like(ref)


def project_block(after, where, h_all, w_qkv, cos, sin):
    def weight(part):
        return pl.BlockSpec((None, D, WIDE), lambda i, where: (2, 0, part * N_HEADS_WIDE + where[0]))

    rows = pl.BlockSpec((512, WIDE), lambda i, *_: (i, 0))
    table = pl.BlockSpec((512, 128), lambda i, *_: (i, 0))
    shape = jax.ShapeDtypeStruct((SEQ, WIDE), BF16)
    return pl.pallas_call(
        project_kernel,
        grid_spec=pltpu.PrefetchScalarGridSpec(
            num_scalar_prefetch=1,
            grid=(SEQ // 512,),
            in_specs=[pl.BlockSpec(memory_space=pl.ANY), pl.BlockSpec((512, D), lambda i, *_: (i, 0)), weight(0), weight(1), weight(2), table, table],
            out_specs=[rows, pl.BlockSpec((WIDE, 512), lambda i, *_: (0, i)), rows],
        ),
        out_shape=[shape, jax.ShapeDtypeStruct((WIDE, SEQ), BF16), shape],
        cost_estimate=cost(2 * SEQ * D * 3 * WIDE, 2 * SEQ * D),
        name="global_qkv",
    )(where, after, h_all, w_qkv, w_qkv, w_qkv, cos, sin)


def global_kernel(where, q, k_t, v, out, s_even, s_odd, m_ref, l_ref, acc_ref):
    length = where[1]
    start = pl.program_id(0) * GQ
    low = lax.broadcasted_iota(jnp.int32, (1, 128), 1) < HEAD_DIM
    scores = (s_even, s_odd)

    def head_step(following, current, top):
        if following is not None:
            cols = slice((following // 2) * 128, (following // 2) * 128 + 128)
            qp = q[:, cols]
            qn = jnp.where(low == (following % 2 == 0), qp, jnp.zeros_like(qp))
            m_ref[...] = jnp.full_like(m_ref, -jnp.inf)
        if current is not None:
            v_cols = slice((current // 2) * 128, (current // 2) * 128 + 128)
            l_ref[...] = jnp.zeros_like(l_ref)
            acc_ref[current % 2] = jnp.zeros((GQ, 128), F32)

        def chunk(c, masked):
            keys = pl.ds(pl.multiple_of(c * GK, GK), GK)
            if following is not None:
                s = dot(qn, k_t[cols, keys])
                if masked:
                    pos = c * GK + lax.broadcasted_iota(jnp.int32, (1, GK), 1)
                    s = s + jnp.where(pos < length, 0.0, NEG)
                scores[following % 2][:, keys] = s
                best = s[:, :128]
                for g in range(1, GK // 128):
                    best = jnp.maximum(best, s[:, g * 128:(g + 1) * 128])
                m_ref[...] = jnp.maximum(m_ref[...], best)
            if current is not None:
                e = jnp.exp(scores[current % 2][:, keys] - top)
                part = e[:, :128]
                for g in range(1, GK // 128):
                    part = part + e[:, g * 128:(g + 1) * 128]
                l_ref[...] += part
                acc_ref[current % 2] += dot(e.astype(BF16), v[keys, v_cols])

        def full_chunk(c, carry):
            chunk(c, False)
            return carry

        n_full = length // GK
        lax.fori_loop(0, n_full, full_chunk, 0)

        @pl.when(n_full * GK < length)
        def _():
            chunk(n_full, True)

        if current is not None:
            acc_ref[current % 2] *= 1.0 / jnp.sum(l_ref[...], axis=1, keepdims=True)
        return None if following is None else jnp.max(m_ref[...], axis=1, keepdims=True)

    @pl.when(start >= length)
    def _():
        out[...] = jnp.zeros_like(out)

    @pl.when(start < length)
    def _():
        ok = start + lax.broadcasted_iota(jnp.int32, (GQ, 1), 0) < length
        top = head_step(0, None, None)
        for head in range(4):
            top = head_step(head + 1 if head < 3 else None, head, top)
            if head % 2 == 1:
                o = jnp.where(low, acc_ref[0], acc_ref[1])
                out[:, (head // 2) * 128:(head // 2) * 128 + 128] = jnp.where(ok, o, 0.0).astype(BF16)


def global_block(where, q, k_t, v):
    rows = pl.BlockSpec((GQ, WIDE), lambda i, *_: (i, 0))
    return pl.pallas_call(
        global_kernel,
        grid_spec=pltpu.PrefetchScalarGridSpec(
            num_scalar_prefetch=1,
            grid=(SEQ // GQ,),
            in_specs=[rows, whole((WIDE, SEQ)), whole((SEQ, WIDE))],
            out_specs=rows,
            scratch_shapes=[pltpu.VMEM((GQ, SEQ), F32)] * 2 + [pltpu.VMEM((GQ, 128), F32)] * 2 + [pltpu.VMEM((2, GQ, 128), F32)],
        ),
        out_shape=jax.ShapeDtypeStruct((SEQ, WIDE), BF16),
        cost_estimate=cost(50e9, 8 * SEQ * WIDE),
        compiler_params=pltpu.CompilerParams(vmem_limit_bytes=VMEM_LIMIT),
        name="global_attn",
    )(where, q, k_t, v)


def solution(mesh):
    to_next = [(d, d + 1) for d in range(GROUP - 1)]
    to_prev = [(d + 1, d) for d in range(GROUP - 1)]

    def layers(hidden, lengths, w_qkv, w_out, w_in, w_mlp_out, attn_gamma, mlp_gamma):
        weights = (w_qkv, w_out, w_in, w_mlp_out, attn_gamma, mlp_gamma)
        me = lax.axis_index('cp').astype(jnp.int32)
        offset = me * ROWS
        cos_l, sin_l = rope_tables(offset + jnp.arange(ROWS), THETA_LOCAL)
        cos_g, sin_g = rope_tables(jnp.arange(SEQ), THETA_GLOBAL)
        at = me[None]
        n_docs = hidden.shape[0]

        docs = range(n_docs)
        xs = [hidden[doc] for doc in docs]
        wheres = [jnp.stack([offset, lengths[doc]]) for doc in docs]
        qkvs, edges, gathered = [None] * n_docs, [None] * n_docs, [None] * n_docs
        last = lengths

        def exchange(doc, qkv):
            qkvs[doc] = qkv
            prev = lax.ppermute(qkv[ROWS - HALO:, D:], 'cp', to_next)
            edges[doc] = prev, lax.ppermute(qkv[:HALO, D:], 'cp', to_prev)

        for doc in docs:
            last = first_block(last, xs[doc], w_qkv, attn_gamma, cos_l, sin_l, 0)
            exchange(doc, last)
        for layer, doc in ((0, 0), (0, 1), (1, 0), (0, 2), (1, 1), (1, 2)):
            o = local_block(last, wheres[doc], qkvs[doc], *edges[doc])
            if layer == 0:
                xs[doc], last = post_block(o, at, [o], xs[doc], weights, 0, "qkv", cos_l, sin_l)
                exchange(doc, last)
            else:
                xs[doc], last = post_block(o, at, [o], xs[doc], weights, 1, "norm")
                gathered[doc] = lax.all_gather(last, 'cp', axis=0, tiled=True)

        attended = []
        for doc in docs:
            where = jnp.stack([jnp.minimum(me, OWNERS - 1), lengths[doc]])
            q, k_t, v = project_block(last, where, gathered[doc], w_qkv, cos_g, sin_g)
            last = global_block(where, q, k_t, v)
            attended.append(last.reshape(GROUP, ROWS, WIDE))

        outs = []
        for lo, hi in ((0, n_docs - 1), (n_docs - 1, n_docs)):
            parts = []
            for k_off in range(GROUP):
                target = lax.rem(me + k_off, GROUP)
                piece = jnp.concatenate([lax.dynamic_index_in_dim(o, target, 0, keepdims=False) for o in attended[lo:hi]], axis=0)
                pairs = [(d, (d + k_off) % GROUP) for d in range(OWNERS)]
                parts.append(lax.ppermute(piece, 'cp', pairs) if k_off else piece)
            x, = post_block(last, at, parts, jnp.concatenate(xs[lo:hi], axis=0), weights, 2, "last")
            outs.append(x)
            last = x
        return jnp.concatenate(outs, axis=0).reshape(n_docs, ROWS, D)

    act_spec = P('dp', 'cp', None)
    return jax.shard_map(layers, mesh=mesh, in_specs=(act_spec, P('dp'), P(), P(), P(), P(), P(), P()), out_specs=act_spec, check_vma=False)
```

time: 1870 us -> 850 us (0.45)
  matrix products: 844 us -> 0 us
  Pallas kernels: 0 us -> 675 us
  waiting for transfers between devices: 567 us -> 2.55 us
  local copies, waits for them, and re-layouts: 229 us -> 26 us
  other arithmetic: 170 us -> 29.6 us
  starting transfers between devices: 34.9 us -> 95.1 us
    pallas_call x0 -> x23, Pallas kernels: none -> 675 us  [the longest x8 327 us: post_block(): pl.pallas_call(functools.partial(post_kernel, layer, mode, n_o), grid_spe...]
    dot_general x19 -> x0, matrix products: 663 us -> none  [the longest x3 187 us: mlp_block(): jnp.einsum('bsf,fd->bsd', gated_act, w_mlp_out_layer, preferred_element_t...]
    all_gather x1 -> x3, waiting for transfers between devices: 563 us -> 0.02 us  [layers(): gathered[doc] = lax.all_gather(last, 'cp', axis=0, tiled=True)]
    sub x3 -> x0, matrix products: 181 us -> none  [masked_softmax(): exp_scores = jnp.exp(scores - row_max)]
    convert_element_type x9 -> x0, local copies, waits for them, and re-layouts: 120 us -> none  [the longest x6 70.6 us: finish_rows(): return jnp.where(row_ok, attn_out, 0.0).astype(jnp.bfloat16)]
    sub x2 -> x0, other arithmetic: 77.4 us -> none  [masked_softmax(): exp_scores = jnp.exp(scores - row_max)]
    ppermute x4 -> x26, starting transfers between devices: 34.9 us -> 95 us  [the longest x14 58.2 us: layers(): parts.append(lax.ppermute(piece, 'cp', pairs) if k_off else piece)]
    unnamed x4 -> x0, other arithmetic: 37.9 us -> none
  transfers between devices with their start and end apart: 5 -> 29, of which waited for: 3 -> 2; matrix products, arithmetic and copies ran while one was open for 2% -> 4% of each run, Pallas kernels for 0% -> 69%
where the time goes in v1:
time: 850 us; the launch traced here: 842 us
  Pallas kernels  675 us (79%)
  starting transfers between devices  95.1 us (11%)
  other arithmetic  29.6 us (3%)
  local copies, waits for them, and re-layouts  26 us (3%)
  between operations  14 us (2%)
    pallas_call x8, Pallas kernels, post_block(): pl.pallas_call(functools.partial(post_kernel, layer, mode, n_o), grid_spe...  327 us
    pallas_call x3, Pallas kernels, global_block(): pl.pallas_call(global_kernel, grid_spec=pltpu.PrefetchScalarGridSpec(num_...  182 us
    pallas_call x3, Pallas kernels, first_block(): pl.pallas_call(functools.partial(first_kernel, layer), grid=(N_QKV,), in_...  63.9 us
    pallas_call x6, Pallas kernels, local_block(): pl.pallas_call(local_kernel, grid_spec=pltpu.PrefetchScalarGridSpec(num_s...  59.9 us
    ppermute x14, starting transfers between devices, layers(): parts.append(lax.ppermute(piece, 'cp', pairs) if k_off else piece)  58.2 us
    pallas_call x3, Pallas kernels, project_block(): pl.pallas_call(project_kernel, grid_spec=pltpu.PrefetchScalarGridSpec(num...  42.6 us
    ppermute x6, starting transfers between devices, exchange(): prev = lax.ppermute(qkv[ROWS - HALO:, D:], 'cp', to_next)  29 us
  transfers between devices with their start and end apart: 29, of which 2 were waited for; matrix products, arithmetic and copies ran while one was open for 4% of the time, Pallas kernels for 69%

profile of v1, /device:TPU:0, one launch (start us, length us, event | category | flops | bytes accessed | tf_op | source)
XLA Modules:
  0.0 842.1 jit_solution(14308575850502800732)
XLA Ops:
  12.7 21.3 %first_qkv.3.after.q.k.v = bf16[384,5376]{1,0:T(8,128)(2,1)} custom-call(s32[3]{0:T(128)} %after.1, bf16[384,1792]{1,0:T(8,128)(2,1)} %get-tuple-element.60.x.refs_3_, bf16[3,1792,5376]{2,1,0:T(8,128)(2,1)} %wv.5, f32[3,1792]{1,0:T(4,128)} %refs_8_.11, f32[384,128]{1,0:T(8,128)} %get-tuple-element.95.cos.refs_10_, f32[384,128]{1,0:T(8,128)} %get-tuple-element.96.sin.refs_11_), custom_call_target="tpu_custom_call" | custom-call | flops 73987520 | bytes 19267584 | tf_op jit(solution)/shard_map/first_qkv/pallas_call | solution.py:126
  40.6 21.4 %first_qkv.4.after.q.k.v = bf16[384,5376]{1,0:T(8,128)(2,1)} custom-call(bf16[384,5376]{1,0:T(8,128)(2,1)} %first_qkv.3.after.q.k.v, bf16[384,1792]{1,0:T(8,128)(2,1)} %get-tuple-element.61.x.refs_3_, bf16[3,1792,5376]{2,1,0:T(8,128)(2,1)} %wv.5, f32[3,1792]{1,0:T(4,128)} %refs_8_.11, f32[384,128]{1,0:T(8,128)} %get-tuple-element.95.cos.refs_10_, ...), custom_call_target="tpu_custom_call" | custom-call | flops 73987520 | bytes 19267584 | tf_op jit(solution)/shard_map/first_qkv/pallas_call | solution.py:126
  69.9 21.3 %first_qkv.5.after.q.k.v = bf16[384,5376]{1,0:T(8,128)(2,1)} custom-call(bf16[384,5376]{1,0:T(8,128)(2,1)} %first_qkv.4.after.q.k.v, bf16[384,1792]{1,0:T(8,128)(2,1)} %get-tuple-element.59.x.refs_3_, bf16[3,1792,5376]{2,1,0:T(8,128)(2,1)} %wv.5, f32[3,1792]{1,0:T(4,128)} %refs_8_.11, f32[384,128]{1,0:T(8,128)} %get-tuple-element.95.cos.refs_10_, ...), custom_call_target="tpu_custom_call" | custom-call | flops 73987520 | bytes 19267584 | tf_op jit(solution)/shard_map/first_qkv/pallas_call | solution.py:126
  93.1 9.7 %local_attn.6.refs_1_.refs_2_ = bf16[384,1792]{1,0:T(8,128)(2,1)} custom-call(s32[2]{0:T(128)} %pad_add_fusion.4.where, bf16[384,5376]{1,0:T(8,128)(2,1)} %first_qkv.5.after.q.k.v, bf16[384,5376]{1,0:T(8,128)(2,1)} %first_qkv.3.after.q.k.v, bf16[384,5376]{1,0:T(8,128)(2,1)} %first_qkv.3.after.q.k.v, bf16[384,5376]{1,0:T(8,128)(2,1)} %first_qkv.3.after.q.k.v, ...), custom_call_target="tpu_custom_call" | custom-call | flops 57600000 | bytes 4128768 | tf_op jit(solution)/shard_map/local_attn/pallas_call | solution.py:369
  102.8 48.7 %shard_map.82 = (bf16[384,1792]{1,0:T(8,128)(2,1)}, bf16[384,5376]{1,0:T(8,128)(2,1)}) custom-call(s32[1]{0:T(128)} %bitcast.refs_0_, bf16[384,1792]{1,0:T(8,128)(2,1)} %local_attn.6.refs_1_.refs_2_, bf16[384,1792]{1,0:T(8,128)(2,1)} %local_attn.6.refs_1_.refs_2_, bf16[384,1792]{1,0:T(8,128)(2,1)} %get-tuple-element.60.x.refs_3_, ...), custom_call_target="tpu_custom_call" | custom-call | flops 257194720 | bytes 66977792 | tf_op jit(solution)/shard_map/pallas_call | solution.py:315
  162.8 10.0 %local_attn.7.refs_1_.refs_2_ = bf16[384,1792]{1,0:T(8,128)(2,1)} custom-call(s32[2]{0:T(128)} %pad_add_fusion.2.where, bf16[384,5376]{1,0:T(8,128)(2,1)} %get-tuple-element.26.after.q.k.v, bf16[384,5376]{1,0:T(8,128)(2,1)} %first_qkv.4.after.q.k.v, bf16[384,5376]{1,0:T(8,128)(2,1)} %first_qkv.4.after.q.k.v, bf16[384,5376]{1,0:T(8,128)(2,1)} %first_qkv.4.after.q.k.v, ...), custom_call_target="tpu_custom_call" | custom-call | flops 57600000 | bytes 4128768 | tf_op jit(solution)/shard_map/local_attn/pallas_call | solution.py:369
  172.8 48.6 %shard_map.83 = (bf16[384,1792]{1,0:T(8,128)(2,1)}, bf16[384,5376]{1,0:T(8,128)(2,1)}) custom-call(s32[1]{0:T(128)} %bitcast.refs_0_, bf16[384,1792]{1,0:T(8,128)(2,1)} %local_attn.7.refs_1_.refs_2_, bf16[384,1792]{1,0:T(8,128)(2,1)} %local_attn.7.refs_1_.refs_2_, bf16[384,1792]{1,0:T(8,128)(2,1)} %get-tuple-element.61.x.refs_3_, ...), custom_call_target="tpu_custom_call" | custom-call | flops 257194720 | bytes 66977792 | tf_op jit(solution)/shard_map/pallas_call | solution.py:315
  221.4 10.2 %local_attn.8.refs_1_.refs_2_ = bf16[384,1792]{1,0:T(8,128)(2,1)} custom-call(s32[2]{0:T(128)} %pad_add_fusion.4.where, bf16[384,5376]{1,0:T(8,128)(2,1)} %get-tuple-element.27.after.q.k.v, bf16[384,5376]{1,0:T(8,128)(2,1)} %get-tuple-element.26.after.q.k.v, bf16[384,5376]{1,0:T(8,128)(2,1)} %get-tuple-element.26.after.q.k.v, ...), custom_call_target="tpu_custom_call" | custom-call | flops 57600000 | bytes 4128768 | tf_op jit(solution)/shard_map/local_attn/pallas_call | solution.py:369
  231.6 32.5 %shard_map.84 = (bf16[384,1792]{1,0:T(8,128)(2,1)}, bf16[384,1792]{1,0:T(8,128)(2,1)}) custom-call(s32[1]{0:T(128)} %bitcast.refs_0_, bf16[384,1792]{1,0:T(8,128)(2,1)} %local_attn.8.refs_1_.refs_2_, bf16[384,1792]{1,0:T(8,128)(2,1)} %local_attn.8.refs_1_.refs_2_, bf16[384,1792]{1,0:T(8,128)(2,1)} %get-tuple-element.28.refs_3_, ...), custom_call_target="tpu_custom_call" | custom-call | flops 183207200 | bytes 47710208 | tf_op jit(solution)/shard_map/pallas_call | solution.py:315
  280.7 10.0 %local_attn.9.refs_1_.refs_2_ = bf16[384,1792]{1,0:T(8,128)(2,1)} custom-call(s32[2]{0:T(128)} %pad_add_fusion.where, bf16[384,1792]{1,0:T(8,128)(2,1)} %get-tuple-element.29.after, bf16[384,5376]{1,0:T(8,128)(2,1)} %first_qkv.5.after.q.k.v, bf16[384,5376]{1,0:T(8,128)(2,1)} %first_qkv.5.after.q.k.v, bf16[384,5376]{1,0:T(8,128)(2,1)} %first_qkv.5.after.q.k.v, ...), custom_call_target="tpu_custom_call" | custom-call | flops 57600000 | bytes 4128768 | tf_op jit(solution)/shard_map/local_attn/pallas_call | solution.py:369
  290.7 48.6 %shard_map.85 = (bf16[384,1792]{1,0:T(8,128)(2,1)}, bf16[384,5376]{1,0:T(8,128)(2,1)}) custom-call(s32[1]{0:T(128)} %bitcast.refs_0_, bf16[384,1792]{1,0:T(8,128)(2,1)} %local_attn.9.refs_1_.refs_2_, bf16[384,1792]{1,0:T(8,128)(2,1)} %local_attn.9.refs_1_.refs_2_, bf16[384,1792]{1,0:T(8,128)(2,1)} %get-tuple-element.59.x.refs_3_, ...), custom_call_target="tpu_custom_call" | custom-call | flops 257194720 | bytes 66977792 | tf_op jit(solution)/shard_map/pallas_call | solution.py:315
  340.3 10.1 %local_attn.10.refs_1_.refs_2_ = bf16[384,1792]{1,0:T(8,128)(2,1)} custom-call(s32[2]{0:T(128)} %pad_add_fusion.2.where, bf16[384,5376]{1,0:T(8,128)(2,1)} %get-tuple-element.30.after.q.k.v, bf16[384,5376]{1,0:T(8,128)(2,1)} %get-tuple-element.27.after.q.k.v, bf16[384,5376]{1,0:T(8,128)(2,1)} %get-tuple-element.27.after.q.k.v, ...), custom_call_target="tpu_custom_call" | custom-call | flops 57600000 | bytes 4128768 | tf_op jit(solution)/shard_map/local_attn/pallas_call | solution.py:369
  350.4 32.6 %shard_map.86 = (bf16[384,1792]{1,0:T(8,128)(2,1)}, bf16[384,1792]{1,0:T(8,128)(2,1)}) custom-call(s32[1]{0:T(128)} %bitcast.refs_0_, bf16[384,1792]{1,0:T(8,128)(2,1)} %local_attn.10.refs_1_.refs_2_, bf16[384,1792]{1,0:T(8,128)(2,1)} %local_attn.10.refs_1_.refs_2_, bf16[384,1792]{1,0:T(8,128)(2,1)} %get-tuple-element.31.refs_3_, ...), custom_call_target="tpu_custom_call" | custom-call | flops 183207200 | bytes 47710208 | tf_op jit(solution)/shard_map/pallas_call | solution.py:315
  397.4 10.0 %local_attn.11.refs_1_.refs_2_ = bf16[384,1792]{1,0:T(8,128)(2,1)} custom-call(s32[2]{0:T(128)} %pad_add_fusion.where, bf16[384,1792]{1,0:T(8,128)(2,1)} %get-tuple-element.32.after, bf16[384,5376]{1,0:T(8,128)(2,1)} %get-tuple-element.30.after.q.k.v, bf16[384,5376]{1,0:T(8,128)(2,1)} %get-tuple-element.30.after.q.k.v, ...), custom_call_target="tpu_custom_call" | custom-call | flops 57600000 | bytes 4128768 | tf_op jit(solution)/shard_map/local_attn/pallas_call | solution.py:369
  407.4 32.7 %shard_map.87 = (bf16[384,1792]{1,0:T(8,128)(2,1)}, bf16[384,1792]{1,0:T(8,128)(2,1)}) custom-call(s32[1]{0:T(128)} %bitcast.refs_0_, bf16[384,1792]{1,0:T(8,128)(2,1)} %local_attn.11.refs_1_.refs_2_, bf16[384,1792]{1,0:T(8,128)(2,1)} %local_attn.11.refs_1_.refs_2_, bf16[384,1792]{1,0:T(8,128)(2,1)} %get-tuple-element.33.refs_3_, ...), custom_call_target="tpu_custom_call" | custom-call | flops 183207200 | bytes 47710208 | tf_op jit(solution)/shard_map/pallas_call | solution.py:315
  453.9 15.2 %global_qkv.3 = (bf16[3072,256]{1,0:T(8,128)(2,1)}, bf16[256,3072]{1,0:T(8,128)(2,1)}, bf16[3072,256]{1,0:T(8,128)(2,1)}) custom-call(s32[2]{0:T(128)} %pad_add_fusion.5.where, bf16[384,1792]{1,0:T(8,128)(2,1)} %get-tuple-element.34.after, bf16[3072,1792]{1,0:T(8,128)(2,1)} %all-gather.4.cloned.1.call-done.h, bf16[3,1792,5376]{2,1,0:T(8,128)(2,1)} %wv.5, ...), custom_call_target="tpu_custom_call" | custom-call | flops 84557168 | bytes 11010048 | tf_op jit(solution)/shard_map/global_qkv/pallas_call | solution.py:405
  469.1 60.6 %global_attn.3.after = bf16[3072,256]{1,0:T(8,128)(2,1)} custom-call(s32[2]{0:T(128)} %pad_add_fusion.5.where, bf16[3072,256]{1,0:T(8,128)(2,1)} %get-tuple-element.35.q, bf16[256,3072]{1,0:T(8,128)(2,1)} %get-tuple-element.36.k_t, bf16[3072,256]{1,0:T(8,128)(2,1)} %get-tuple-element.37.v), custom_call_target="tpu_custom_call" | custom-call | flops 500000000 | bytes 6291456 | tf_op jit(solution)/shard_map/global_attn/pallas_call | solution.py:488
  529.7 13.8 %global_qkv.4 = (bf16[3072,256]{1,0:T(8,128)(2,1)}, bf16[256,3072]{1,0:T(8,128)(2,1)}, bf16[3072,256]{1,0:T(8,128)(2,1)}) custom-call(s32[2]{0:T(128)} %pad_add_fusion.3.where, bf16[3072,256]{1,0:T(8,128)(2,1)} %global_attn.3.after, bf16[3072,1792]{1,0:T(8,128)(2,1)} %all-gather.6.cloned.1.call-done.h, bf16[3,1792,5376]{2,1,0:T(8,128)(2,1)} %wv.5, ...), custom_call_target="tpu_custom_call" | custom-call | flops 84557168 | bytes 11010048 | tf_op jit(solution)/shard_map/global_qkv/pallas_call | solution.py:405
  543.5 60.8 %global_attn.4.after = bf16[3072,256]{1,0:T(8,128)(2,1)} custom-call(s32[2]{0:T(128)} %pad_add_fusion.3.where, bf16[3072,256]{1,0:T(8,128)(2,1)} %get-tuple-element.38.q, bf16[256,3072]{1,0:T(8,128)(2,1)} %get-tuple-element.39.k_t, bf16[3072,256]{1,0:T(8,128)(2,1)} %get-tuple-element.40.v), custom_call_target="tpu_custom_call" | custom-call | flops 500000000 | bytes 6291456 | tf_op jit(solution)/shard_map/global_attn/pallas_call | solution.py:488
  606.4 17.6 %collective-permute-start.12 = (bf16[768,256]{1,0:T(8,128)(2,1)S(1)}, bf16[768,256]{1,0:T(8,128)(2,1)S(1)}, u32[]{:S(2)}, u32[]{:S(2)}) collective-permute-start(bf16[768,256]{1,0:T(8,128)(2,1)S(1)} %pad_maximum_fusion.5), channel_id=1, source_target_pairs={{0,1},{1,2},{2,3},{3,4},{4,5},{5,6},{6,7},{8,9},{9,10},{10,11},{11... | collective-permute-start | bytes 1179656 | tf_op jit(solution)/shard_map/ppermute | solution.py:554
  641.9 13.6 %global_qkv.5 = (bf16[3072,256]{1,0:T(8,128)(2,1)}, bf16[256,3072]{1,0:T(8,128)(2,1)}, bf16[3072,256]{1,0:T(8,128)(2,1)}) custom-call(s32[2]{0:T(128)} %pad_add_fusion.1.where, bf16[3072,256]{1,0:T(8,128)(2,1)} %global_attn.4.after, bf16[3072,1792]{1,0:T(8,128)(2,1)} %all-gather.8.cloned.1.call-done.h, bf16[3,1792,5376]{2,1,0:T(8,128)(2,1)} %wv.5, ...), custom_call_target="tpu_custom_call" | custom-call | flops 84557168 | bytes 11010048 | tf_op jit(solution)/shard_map/global_qkv/pallas_call | solution.py:405
  660.0 60.2 %global_attn.5.refs_1_ = bf16[3072,256]{1,0:T(8,128)(2,1)} custom-call(s32[2]{0:T(128)} %pad_add_fusion.1.where, bf16[3072,256]{1,0:T(8,128)(2,1)} %get-tuple-element.41.q, bf16[256,3072]{1,0:T(8,128)(2,1)} %get-tuple-element.42.k_t, bf16[3072,256]{1,0:T(8,128)(2,1)} %get-tuple-element.43.v), custom_call_target="tpu_custom_call" | custom-call | flops 500000000 | bytes 6291456 | tf_op jit(solution)/shard_map/global_attn/pallas_call | solution.py:488
  747.1 53.4 %shard_map.88.refs_1_ = bf16[768,1792]{1,0:T(8,128)(2,1)} custom-call(s32[1]{0:T(128)} %bitcast.refs_0_, bf16[3072,256]{1,0:T(8,128)(2,1)} %global_attn.5.refs_1_, bf16[768,256]{1,0:T(8,128)(2,1)} %pad_maximum_fusion.4.refs_2_, bf16[768,256]{1,0:T(8,128)(2,1)} %copy-done.11, bf16[768,256]{1,0:T(8,128)(2,1)} %copy-done.12, ...), custom_call_target="tpu_custom_call" | custom-call | flops 366414400 | bytes 47710208 | tf_op jit(solution)/shard_map/pallas_call | solution.py:315
  801.3 29.6 %shard_map.89 = bf16[384,1792]{1,0:T(8,128)(2,1)} custom-call(s32[1]{0:T(128)} %bitcast.refs_0_, bf16[768,1792]{1,0:T(8,128)(2,1)} %shard_map.88.refs_1_, bf16[384,256]{1,0:T(8,128)(2,1)} %get-tuple-element.69.refs_2_, bf16[384,256]{1,0:T(8,128)(2,1)} %copy-done.13, bf16[384,256]{1,0:T(8,128)(2,1)} %copy-done.14, ...), custom_call_target="tpu_custom_call" | custom-call | flops 183207200 | bytes 47710208 | tf_op jit(solution)/shard_map/pallas_call | solution.py:315
  (131 shorter events, 135.7 us)
Async XLA Ops:
  6.5 447.4 %all-gather.4.cloned.1.call-start = ((), (), s32[]{:S(2)}) async-start(), calls=%async_computation | async-start | bytes 12386304 | tf_op jit(solution)/shard_map/all_gather | solution.py:538
  36.1 57.0 %collective-permute-start = (bf16[64,3584]{1,0:T(8,128)(2,1)}, bf16[64,3584]{1,0:T(8,128)(2,1)}, u32[]{:S(2)}, u32[]{:S(2)}) collective-permute-start(bf16[64,3584]{1,0:T(8,128)(2,1)} %get-tuple-element.58), channel_id=1, source_target_pairs={{0,1},{1,2},{2,3},{3,4},{4,5},{5,6},{6,7},{8,9},{9,10},{10,11},{11... | collective-permute-start | bytes 1376264 | tf_op jit(solution)/shard_map/ppermute | solution.py:525
  39.3 53.8 %collective-permute-start.1 = (bf16[64,3584]{1,0:T(8,128)(2,1)}, bf16[64,3584]{1,0:T(8,128)(2,1)}, u32[]{:S(2)}, u32[]{:S(2)}) collective-permute-start(bf16[64,3584]{1,0:T(8,128)(2,1)} %get-tuple-element.57), channel_id=1, source_target_pairs={{1,0},{2,1},{3,2},{4,3},{5,4},{6,5},{7,6},{9,8},{10,9},{11,10},{12... | collective-permute-start | bytes 1376264 | tf_op jit(solution)/shard_map/ppermute | solution.py:526
  64.1 97.2 %collective-permute-start.2 = (bf16[64,3584]{1,0:T(8,128)(2,1)}, bf16[64,3584]{1,0:T(8,128)(2,1)S(1)}, u32[]{:S(2)}, u32[]{:S(2)}) collective-permute-start(bf16[64,3584]{1,0:T(8,128)(2,1)} %get-tuple-element.56), channel_id=1, source_target_pairs={{0,1},{1,2},{2,3},{3,4},{4,5},{5,6},{6,7},{8,9},{9,10},{10,11},{11... | collective-permute-start | bytes 1376264 | tf_op jit(solution)/shard_map/ppermute | solution.py:525
  68.6 92.7 %collective-permute-start.3 = (bf16[64,3584]{1,0:T(8,128)(2,1)}, bf16[64,3584]{1,0:T(8,128)(2,1)S(1)}, u32[]{:S(2)}, u32[]{:S(2)}) collective-permute-start(bf16[64,3584]{1,0:T(8,128)(2,1)} %get-tuple-element.55), channel_id=1, source_target_pairs={{1,0},{2,1},{3,2},{4,3},{5,4},{6,5},{7,6},{9,8},{10,9},{11,10},{12... | collective-permute-start | bytes 1376264 | tf_op jit(solution)/shard_map/ppermute | solution.py:526
  153.7 67.7 %collective-permute-start.4 = (bf16[64,3584]{1,0:T(8,128)(2,1)}, bf16[64,3584]{1,0:T(8,128)(2,1)}, u32[]{:S(2)}, u32[]{:S(2)}) collective-permute-start(bf16[64,3584]{1,0:T(8,128)(2,1)} %get-tuple-element.54), channel_id=1, source_target_pairs={{0,1},{1,2},{2,3},{3,4},{4,5},{5,6},{6,7},{8,9},{9,10},{10,11},{11... | collective-permute-start | bytes 1376264 | tf_op jit(solution)/shard_map/ppermute | solution.py:525
  158.7 62.7 %collective-permute-start.5 = (bf16[64,3584]{1,0:T(8,128)(2,1)}, bf16[64,3584]{1,0:T(8,128)(2,1)}, u32[]{:S(2)}, u32[]{:S(2)}) collective-permute-start(bf16[64,3584]{1,0:T(8,128)(2,1)} %get-tuple-element.53), channel_id=1, source_target_pairs={{1,0},{2,1},{3,2},{4,3},{5,4},{6,5},{7,6},{9,8},{10,9},{11,10},{12... | collective-permute-start | bytes 1376264 | tf_op jit(solution)/shard_map/ppermute | solution.py:526
  264.1 265.6 %all-gather.6.cloned.1.call-start = ((), (), s32[]{:S(2)}) async-start(), calls=%async_computation.1 | async-start | bytes 12386304 | tf_op jit(solution)/shard_map/all_gather | solution.py:538
  272.4 67.0 %collective-permute-start.8 = (bf16[64,3584]{1,0:T(8,128)(2,1)}, bf16[64,3584]{1,0:T(8,128)(2,1)S(1)}, u32[]{:S(2)}, u32[]{:S(2)}) collective-permute-start(bf16[64,3584]{1,0:T(8,128)(2,1)} %get-tuple-element.50), channel_id=1, source_target_pairs={{0,1},{1,2},{2,3},{3,4},{4,5},{5,6},{6,7},{8,9},{9,10},{10,11},{11... | collective-permute-start | bytes 1376264 | tf_op jit(solution)/shard_map/ppermute | solution.py:525
  276.6 62.7 %collective-permute-start.9 = (bf16[64,3584]{1,0:T(8,128)(2,1)}, bf16[64,3584]{1,0:T(8,128)(2,1)S(1)}, u32[]{:S(2)}, u32[]{:S(2)}) collective-permute-start(bf16[64,3584]{1,0:T(8,128)(2,1)} %get-tuple-element.49), channel_id=1, source_target_pairs={{1,0},{2,1},{3,2},{4,3},{5,4},{6,5},{7,6},{9,8},{10,9},{11,10},{12... | collective-permute-start | bytes 1376264 | tf_op jit(solution)/shard_map/ppermute | solution.py:526
  383.1 258.8 %all-gather.8.cloned.1.call-start = ((), (), s32[]{:S(2)}) async-start(), calls=%async_computation.2 | async-start | bytes 12386304 | tf_op jit(solution)/shard_map/all_gather | solution.py:538
  606.4 49.1 %collective-permute-start.12 = (bf16[768,256]{1,0:T(8,128)(2,1)S(1)}, bf16[768,256]{1,0:T(8,128)(2,1)S(1)}, u32[]{:S(2)}, u32[]{:S(2)}) collective-permute-start(bf16[768,256]{1,0:T(8,128)(2,1)S(1)} %pad_maximum_fusion.5), channel_id=1, source_target_pairs={{0,1},{1,2},{2,3},{3,4},{4,5},{5,6},{6,7},{8,9},{9,10},{10,11},{11... | collective-permute-start | bytes 1179656 | tf_op jit(solution)/shard_map/ppermute | solution.py:554
  624.1 33.9 %collective-permute-start.13 = (bf16[768,256]{1,0:T(8,128)(2,1)S(1)}, bf16[768,256]{1,0:T(8,128)(2,1)S(1)}, u32[]{:S(2)}, u32[]{:S(2)}) collective-permute-start(bf16[768,256]{1,0:T(8,128)(2,1)S(1)} %pad_maximum_fusion.6), channel_id=1, source_target_pairs={{0,2},{1,3},{2,4},{3,5},{4,6},{5,7},{6,0},{8,10},{9,11},{10,12},{1... | collective-permute-start | bytes 1179656 | tf_op jit(solution)/shard_map/ppermute | solution.py:554
  631.1 91.7 %collective-permute-start.14 = (bf16[768,256]{1,0:T(8,128)(2,1)}, bf16[768,256]{1,0:T(8,128)(2,1)}, u32[]{:S(2)}, u32[]{:S(2)}) collective-permute-start(bf16[768,256]{1,0:T(8,128)(2,1)} %pad_maximum_fusion.7), channel_id=1, source_target_pairs={{0,3},{1,4},{2,5},{3,6},{4,7},{5,0},{6,1},{8,11},{9,12},{10,13},{1... | collective-permute-start | bytes 1179656 | tf_op jit(solution)/shard_map/ppermute | solution.py:554
  633.8 91.4 %collective-permute-start.15 = (bf16[768,256]{1,0:T(8,128)(2,1)}, bf16[768,256]{1,0:T(8,128)(2,1)}, u32[]{:S(2)}, u32[]{:S(2)}) collective-permute-start(bf16[768,256]{1,0:T(8,128)(2,1)} %pad_maximum_fusion.8), channel_id=1, source_target_pairs={{0,4},{1,5},{2,6},{3,7},{4,0},{5,1},{6,2},{8,12},{9,13},{10,14},{1... | collective-permute-start | bytes 1179656 | tf_op jit(solution)/shard_map/ppermute | solution.py:554
  636.5 92.1 %collective-permute-start.16 = (bf16[768,256]{1,0:T(8,128)(2,1)}, bf16[768,256]{1,0:T(8,128)(2,1)}, u32[]{:S(2)}, u32[]{:S(2)}) collective-permute-start(bf16[768,256]{1,0:T(8,128)(2,1)} %pad_maximum_fusion.9), channel_id=1, source_target_pairs={{0,5},{1,6},{2,7},{3,0},{4,1},{5,2},{6,3},{8,13},{9,14},{10,15},{1... | collective-permute-start | bytes 1179656 | tf_op jit(solution)/shard_map/ppermute | solution.py:554
  655.5 78.0 %collective-permute-start.17 = (bf16[768,256]{1,0:T(8,128)(2,1)}, bf16[768,256]{1,0:T(8,128)(2,1)}, u32[]{:S(2)}, u32[]{:S(2)}) collective-permute-start(bf16[768,256]{1,0:T(8,128)(2,1)} %pad_maximum_fusion.10), channel_id=1, source_target_pairs={{0,6},{1,7},{2,0},{3,1},{4,2},{5,3},{6,4},{8,14},{9,15},{10,8},{11... | collective-permute-start | bytes 1179656 | tf_op jit(solution)/shard_map/ppermute | solution.py:554
  658.0 77.4 %collective-permute-start.18 = (bf16[768,256]{1,0:T(8,128)(2,1)S(1)}, bf16[768,256]{1,0:T(8,128)(2,1)}, u32[]{:S(2)}, u32[]{:S(2)}) collective-permute-start(bf16[768,256]{1,0:T(8,128)(2,1)S(1)} %pad_maximum_fusion.11), channel_id=1, source_target_pairs={{0,7},{1,0},{2,1},{3,2},{4,3},{5,4},{6,5},{8,15},{9,8},{10,9},{11,... | collective-permute-start | bytes 1179656 | tf_op jit(solution)/shard_map/ppermute | solution.py:554
  725.2 17.4 %collective-permute-start.20 = (bf16[384,256]{1,0:T(8,128)(2,1)S(1)}, bf16[384,256]{1,0:T(8,128)(2,1)S(1)}, u32[]{:S(2)}, u32[]{:S(2)}) collective-permute-start(bf16[384,256]{1,0:T(8,128)(2,1)S(1)} %get-tuple-element.67), channel_id=1, source_target_pairs={{0,2},{1,3},{2,4},{3,5},{4,6},{5,7},{6,0},{8,10},{9,11},{10,12},{1... | collective-permute-start | bytes 589832 | tf_op jit(solution)/shard_map/ppermute | solution.py:554
  728.6 72.0 %collective-permute-start.21 = (bf16[384,256]{1,0:T(8,128)(2,1)}, bf16[384,256]{1,0:T(8,128)(2,1)}, u32[]{:S(2)}, u32[]{:S(2)}) collective-permute-start(bf16[384,256]{1,0:T(8,128)(2,1)} %get-tuple-element.66), channel_id=1, source_target_pairs={{0,3},{1,4},{2,5},{3,6},{4,7},{5,0},{6,1},{8,11},{9,12},{10,13},{1... | collective-permute-start | bytes 589832 | tf_op jit(solution)/shard_map/ppermute | solution.py:554
  733.5 67.1 %collective-permute-start.22 = (bf16[384,256]{1,0:T(8,128)(2,1)}, bf16[384,256]{1,0:T(8,128)(2,1)}, u32[]{:S(2)}, u32[]{:S(2)}) collective-permute-start(bf16[384,256]{1,0:T(8,128)(2,1)} %get-tuple-element.65), channel_id=1, source_target_pairs={{0,4},{1,5},{2,6},{3,7},{4,0},{5,1},{6,2},{8,12},{9,13},{10,14},{1... | collective-permute-start | bytes 589832 | tf_op jit(solution)/shard_map/ppermute | solution.py:554
  735.5 65.1 %collective-permute-start.23 = (bf16[384,256]{1,0:T(8,128)(2,1)}, bf16[384,256]{1,0:T(8,128)(2,1)S(1)}, u32[]{:S(2)}, u32[]{:S(2)}) collective-permute-start(bf16[384,256]{1,0:T(8,128)(2,1)} %get-tuple-element.64), channel_id=1, source_target_pairs={{0,5},{1,6},{2,7},{3,0},{4,1},{5,2},{6,3},{8,13},{9,14},{10,15},{1... | collective-permute-start | bytes 589832 | tf_op jit(solution)/shard_map/ppermute | solution.py:554
  739.8 60.9 %collective-permute-start.24 = (bf16[384,256]{1,0:T(8,128)(2,1)}, bf16[384,256]{1,0:T(8,128)(2,1)S(1)}, u32[]{:S(2)}, u32[]{:S(2)}) collective-permute-start(bf16[384,256]{1,0:T(8,128)(2,1)} %get-tuple-element.63), channel_id=1, source_target_pairs={{0,6},{1,7},{2,0},{3,1},{4,2},{5,3},{6,4},{8,14},{9,15},{10,8},{11... | collective-permute-start | bytes 589832 | tf_op jit(solution)/shard_map/ppermute | solution.py:554
  742.6 58.0 %collective-permute-start.25 = (bf16[384,256]{1,0:T(8,128)(2,1)S(1)}, bf16[384,256]{1,0:T(8,128)(2,1)}, u32[]{:S(2)}, u32[]{:S(2)}) collective-permute-start(bf16[384,256]{1,0:T(8,128)(2,1)S(1)} %get-tuple-element.62), channel_id=1, source_target_pairs={{0,7},{1,0},{2,1},{3,2},{4,3},{5,4},{6,5},{8,15},{9,8},{10,9},{11,... | collective-permute-start | bytes 589832 | tf_op jit(solution)/shard_map/ppermute | solution.py:554
  (23 other events, 149.3 us)
Sparse Core Ops, SparseCore 0:
  264.3 112.7 all-gather.3
  383.2 111.9 all-gather.5
  496.8 102.0 all-gather.7
